TPU v7x, 32 devices: a whole 2x2x4 slice. The times are simulated.
32 devices in a mesh: dp: 8 (over z, x), blk: 4 (over y, core).
Axes of the slice: x: 2, y: 2, z: 4, core: 2. Of those that a mesh axis runs over, the one named last changes fastest.
Arguments:
- queries: bfloat16 [8, 512, 2048], P('dp', 'blk'), may hold values from -6 to 6
- keys: bfloat16 [8, 512, 512], P('dp', 'blk'), may hold values from -6 to 6
- values: bfloat16 [8, 512, 512], P('dp', 'blk'), may hold values from -6 to 6
- out_grad: bfloat16 [8, 512, 2048], P('dp', 'blk'), may hold values from -6 to 6
- layer_input: bfloat16 [8, 512, 4096], P('dp', 'blk'), may hold values from -6 to 6
- lengths: int32 [8, 3], P('dp'), may hold values from 32 to 448, as said below
Outputs:
- query_grad: bfloat16 [8, 512, 2048], P('dp', 'blk')
- key_grad: bfloat16 [8, 512, 512], P('dp', 'blk')
- value_grad: bfloat16 [8, 512, 512], P('dp', 'blk')
- weight_grad: float32 [4096, 1024], P(('dp', 'blk'))
Inputs may be any that keep to these rules, and one draw needn't show every extreme that they name: `lengths`: each row sums to 512; the chosen and rejected counts lie between 32 and 96.
All inputs are finite; a program needn't handle non-finite values.
Results may differ from a plain program's by a relative error of at most 0.023.
Values may be sent and summed in bfloat16 or wider, within the bound.
A program may use at most 128 MiB of HBM per device.

v0:
```python
import math

import jax
import jax.numpy as jnp
from jax import lax
from jax.sharding import PartitionSpec as P

HEAD = 128


rope_base = 500000.0
masked_fill = -1e30


def stored_positions(stored_rows, shard_rows, shard_count):
    half_rows = shard_rows // 2
    block_number = stored_rows // half_rows
    holder = block_number // 2
    upper_half = block_number % 2
    position_block = jnp.where(upper_half == 1, 2 * shard_count - 1 - holder, holder)
    return (position_block * half_rows + stored_rows % half_rows).astype(jnp.int32)


def allowed_pairs(query_pos, key_pos, prompt_len, chosen_len):
    causal = key_pos[None, :] <= query_pos[:, None]
    reject_start = prompt_len + chosen_len
    query_rejected = query_pos >= reject_start
    key_chosen = jnp.logical_and(key_pos >= prompt_len, key_pos < reject_start)
    return jnp.logical_and(
        causal, jnp.logical_not(jnp.logical_and(query_rejected[:, None], key_chosen[None, :]))
    )


def block_length(total_rows):
    chosen_size = 1
    for candidate in range(1, min(total_rows, 512) + 1):
        if total_rows % candidate == 0:
            chosen_size = candidate
    return chosen_size


def over_blocks(running, pieces, first_row, block_fn):
    total_rows = pieces[0].shape[0]
    block_rows = block_length(total_rows)

    def one_turn(turn_index, current):
        block_start = turn_index * block_rows
        block_parts = tuple(
            (lax.dynamic_slice_in_dim(member, block_start, block_rows, 0) for member in pieces)
        )
        return block_fn(current, block_parts, first_row + block_start)

    return lax.fori_loop(0, total_rows // block_rows, one_turn, running)


def body(queries, keys, values, out_grad, layer_input, lengths):
    shard_count = lax.axis_size("blk")
    shard_index = lax.axis_index("blk")
    shard_rows = queries.shape[1]
    kv_heads = keys.shape[2] // HEAD
    group_heads = queries.shape[2] // keys.shape[2]
    seq_len = shard_rows * shard_count
    query_count = group_heads * shard_rows
    scale = 1.0 / math.sqrt(HEAD)
    prompt_len = lengths[0, 0]
    chosen_len = lengths[0, 1]
    own_rows = shard_index * shard_rows + jnp.arange(shard_rows, dtype=jnp.int32)
    own_pos = stored_positions(own_rows, shard_rows, shard_count)
    query_pos = jnp.tile(own_pos, group_heads)
    query_rows = (
        queries[0]
        .reshape(shard_rows, kv_heads, group_heads, HEAD)
        .transpose(1, 2, 0, 3)
        .reshape(kv_heads, query_count, HEAD)
    )
    grad_rows = (
        out_grad[0]
        .reshape(shard_rows, kv_heads, group_heads, HEAD)
        .transpose(1, 2, 0, 3)
        .reshape(kv_heads, query_count, HEAD)
    )

    def block_allowed(first_row, count_rows):
        key_pos = stored_positions(
            first_row + jnp.arange(count_rows, dtype=jnp.int32), shard_rows, shard_count
        )
        return allowed_pairs(query_pos, key_pos, prompt_len, chosen_len)

    def forward_block(running, block_parts, first_row):
        key_block, value_block = block_parts
        count_rows = key_block.shape[0]
        allowed = block_allowed(first_row, count_rows)
        run_max, run_sum, run_acc = running
        key_heads = key_block.reshape(count_rows, kv_heads, HEAD)
        value_heads = value_block.reshape(count_rows, kv_heads, HEAD).astype(jnp.float32)
        scores = scale * jnp.einsum(
            "gqe,kge->gqk", query_rows, key_heads, preferred_element_type=jnp.float32
        )
        new_max = jnp.maximum(
            run_max, jnp.max(jnp.where(allowed[None], scores, masked_fill), axis=-1)
        )
        weights = jnp.where(allowed[None], jnp.exp(scores - new_max[..., None]), 0.0)
        factor = jnp.exp(run_max - new_max)
        new_sum = run_sum * factor + jnp.sum(weights, axis=-1)
        new_acc = run_acc * factor[..., None] + jnp.einsum(
            "gqk,kge->gqe", weights, value_heads, precision=lax.Precision.HIGHEST
        )
        return (new_max, new_sum, new_acc)

    start_forward = (
        jnp.full((kv_heads, query_count), masked_fill, jnp.float32),
        jnp.zeros((kv_heads, query_count), jnp.float32),
        jnp.zeros((kv_heads, query_count, HEAD), jnp.float32),
    )
    run_max, run_sum, run_acc = over_blocks(
        start_forward,
        (
            lax.all_gather(keys[0], "blk", axis=0, tiled=True),
            lax.all_gather(values[0], "blk", axis=0, tiled=True),
        ),
        jnp.int32(0),
        forward_block,
    )
    attn_out = run_acc / run_sum[..., None]
    log_total = run_max + jnp.log(run_sum)
    delta = jnp.sum(grad_rows.astype(jnp.float32) * attn_out, axis=-1)

    def backward_block(running, block_parts, first_row):
        key_block, value_block = block_parts
        count_rows = key_block.shape[0]
        allowed = block_allowed(first_row, count_rows)
        query_acc, key_acc, value_acc = running
        key_heads = key_block.reshape(count_rows, kv_heads, HEAD)
        value_heads = value_block.reshape(count_rows, kv_heads, HEAD)
        scores = scale * jnp.einsum(
            "gqe,kge->gqk", query_rows, key_heads, preferred_element_type=jnp.float32
        )
        probs = jnp.where(allowed[None], jnp.exp(scores - log_total[..., None]), 0.0)
        prob_half = probs.astype(jnp.bfloat16)
        prob_grad = jnp.einsum(
            "gqe,kge->gqk", grad_rows, value_heads, preferred_element_type=jnp.float32
        )
        score_grad = (scale * probs * (prob_grad - delta[..., None])).astype(jnp.bfloat16)
        query_acc = query_acc + jnp.einsum(
            "gqk,kge->gqe", score_grad, key_heads, preferred_element_type=jnp.float32
        )
        key_term = jnp.einsum(
            "gqk,gqe->kge", score_grad, query_rows, preferred_element_type=jnp.float32
        ).reshape(count_rows, kv_heads * HEAD)
        value_term = jnp.einsum(
            "gqk,gqe->kge", prob_half, grad_rows, preferred_element_type=jnp.float32
        ).reshape(count_rows, kv_heads * HEAD)
        key_acc = lax.dynamic_update_slice_in_dim(
            key_acc,
            lax.dynamic_slice_in_dim(key_acc, first_row, count_rows, 0) + key_term,
            first_row,
            0,
        )
        value_acc = lax.dynamic_update_slice_in_dim(
            value_acc,
            lax.dynamic_slice_in_dim(value_acc, first_row, count_rows, 0) + value_term,
            first_row,
            0,
        )
        return (query_acc, key_acc, value_acc)

    start_backward = (
        jnp.zeros((kv_heads, query_count, HEAD), jnp.float32),
        jnp.zeros((seq_len, kv_heads * HEAD), jnp.float32),
        jnp.zeros((seq_len, kv_heads * HEAD), jnp.float32),
    )
    query_acc, key_acc, value_acc = over_blocks(
        start_backward,
        (
            lax.all_gather(keys[0], "blk", axis=0, tiled=True),
            lax.all_gather(values[0], "blk", axis=0, tiled=True),
        ),
        jnp.int32(0),
        backward_block,
    )
    key_sum, value_sum = (
        lax.psum_scatter(
            key_acc.astype(jnp.bfloat16), "blk", scatter_dimension=0, tiled=True
        ).astype(jnp.float32),
        lax.psum_scatter(
            value_acc.astype(jnp.bfloat16), "blk", scatter_dimension=0, tiled=True
        ).astype(jnp.float32),
    )
    query_grad = (
        query_acc.reshape(kv_heads, group_heads, shard_rows, HEAD)
        .transpose(2, 0, 1, 3)
        .reshape(shard_rows, kv_heads * group_heads * HEAD)
        .astype(jnp.bfloat16)
    )
    key_out = key_sum.astype(jnp.bfloat16)
    value_out = value_sum.astype(jnp.bfloat16)
    half_dim = HEAD // 2
    frequency = jnp.exp(
        -(2.0 * jnp.arange(half_dim, dtype=jnp.float32) / HEAD) * math.log(rope_base)
    )
    angles = own_pos.astype(jnp.float32)[:, None] * frequency[None, :]
    cosine = jnp.concatenate([jnp.cos(angles), jnp.cos(angles)], axis=-1)[:, None, :]
    sine = jnp.concatenate([jnp.sin(angles), jnp.sin(angles)], axis=-1)[:, None, :]
    grad_heads = key_sum.reshape(shard_rows, kv_heads, HEAD)
    rotated = jnp.concatenate([-grad_heads[..., half_dim:], grad_heads[..., :half_dim]], axis=-1)
    key_pre = (
        (grad_heads * cosine - rotated * sine)
        .reshape(shard_rows, kv_heads * HEAD)
        .astype(jnp.bfloat16)
    )
    grad_cols = jnp.concatenate([key_pre, value_out], axis=1)
    input_rows = layer_input[0]
    features = layer_input.shape[2]
    replica_count = lax.axis_size("dp")
    feature_share = features // (replica_count * shard_count)
    grouped_input = input_rows.reshape(shard_rows, replica_count, shard_count * feature_share)
    sequence_input = lax.all_to_all(grouped_input, "blk", split_axis=2, concat_axis=0, tiled=True)
    sequence_weight = jnp.einsum(
        "tif,tc->ifc",
        sequence_input,
        lax.all_gather(grad_cols, "blk", axis=0, tiled=True),
        preferred_element_type=jnp.float32,
    )
    weight_grad = (
        lax.psum_scatter(
            sequence_weight.astype(jnp.bfloat16), "dp", scatter_dimension=0, tiled=True
        )
        .astype(jnp.float32)
        .reshape(feature_share, grad_cols.shape[1])
    )
    return (query_grad[None], key_out[None], value_out[None], weight_grad)


def solution(mesh):
    placed = (
        P("dp", "blk", None),
        P("dp", "blk", None),
        P("dp", "blk", None),
        P("dp", "blk", None),
        P("dp", "blk", None),
        P("dp", None),
    )
    return jax.shard_map(
        body,
        mesh=mesh,
        in_specs=placed,
        out_specs=(
            P("dp", "blk", None),
            P("dp", "blk", None),
            P("dp", "blk", None),
            P(("dp", "blk"), None),
        ),
        check_vma=False,
    )
```

profile of v0, /device:TPU:0, one launch (start us, length us, event | category | flops | bytes accessed | tf_op | source)
XLA Modules:
  0.0 209.5 jit_solution(16172209524626766928)
XLA Ops:
  7.2 0.0 reduce-scatter.10.cloned.1.call-start
  7.2 1.3 fusion.41
  9.9 0.7 compare_and_fusion
  10.6 1.4 reshape_squeeze.9
  12.0 0.6 copy.85
  12.6 0.2 reshape.331
  12.8 1.0 copy.86
  13.8 8.7 %all-gather = bf16[1,512,512]{1,2,0:T(8,128)(2,1)S(1)} all-gather(bf16[1,128,512]{1,2,0:T(8,128)(2,1)S(1)} %copy.86), channel_id=2, replica_groups=mesh['dp'=8,'blk'=4] {'blk'}, dimensions={1}, use_global_device_ids=true | all-gather | bytes 655360 | tf_op jit(solution)/shard_map/all_gather | solution.py:175
  22.5 0.3 not_and_fusion
  22.8 1.0 select_reduce_fusion
  23.8 1.9 copy-done
  25.7 0.9 fusion.1
  26.6 0.4 reshape_squeeze.10
  27.0 0.6 copy.89
  27.6 0.2 reshape.333
  27.8 0.1 copy.90
  28.0 7.3 %all-gather.1 = bf16[1,512,512]{1,2,0:T(8,128)(2,1)S(1)} all-gather(bf16[1,128,512]{1,2,0:T(8,128)(2,1)S(1)} %copy.90), channel_id=3, replica_groups=mesh['dp'=8,'blk'=4] {'blk'}, dimensions={1}, use_global_device_ids=true | all-gather | bytes 655360 | tf_op jit(solution)/shard_map/all_gather | solution.py:176
  35.3 4.9 %multiply_reduce_fusion = f32[4,512]{1,0:T(4,128)S(1)} fusion(bf16[4,512,128]{1,2,0:T(8,128)(2,1)S(1)} %reshape.333, bf16[512,4,128]{0,2,1:T(8,128)(2,1)S(1)} %bitcast.73, f32[4,512,512]{1,2,0:T(8,128)} %copy-done, f32[4,512]{1,0:T(4,128)S(1)} %broadcast_maximum_fusion, pred[512,512]{0,1:T(8,128)(4,1)S(1)} %not_and_fusion, ...), kind=kOutput, calls=%fused_computation.22 | convolution fusion | flops 1615067136 | bytes 5537792 | tf_op jit(solution)/shard_map/while/body/eval_jaxpr/gqk,kge->gqe/dot_general | solution.py:105
  40.2 2.7 %multiply_convert_fusion = bf16[4,512,512]{1,2,0:T(8,128)(2,1)S(1)} fusion(f32[4,512,512]{1,2,0:T(8,128)S(1)} %copy-done.1, bf16[4,512,128]{1,2,0:T(8,128)(2,1)} %copy-done.3, bf16[512,4,128]{0,2,1:T(8,128)(2,1)S(1)} %bitcast.74, f32[4,512]{1,0:T(4,128)S(1)} %multiply_reduce_fusion, f32[4,512]{1,0:T(4,128)S(1)} %get-tuple-element.90, ...), kind=kOutput, calls=%fused_computation | convolution fusion | flops 275775488 | bytes 7618560 | tf_op jit(solution)/shard_map/while/body/eval_jaxpr/gqe,kge->gqk/dot_general | solution.py:140
  42.9 1.6 convolution_convert_fusion
  44.5 2.1 copy.117
  46.6 0.0 reduce-scatter.10.cloned.1.call-update
  46.6 0.0 reduce-scatter.12.cloned.1.call-start
  46.6 3.4 %fusion.14 = bf16[4,512,128]{1,2,0:T(8,128)(2,1)S(1)} fusion(bf16[4,512,128]{1,2,0:T(8,128)(2,1)} %copy-done.3, f32[4,512,512]{1,2,0:T(8,128)} %copy-done, f32[4,512]{1,0:T(4,128)S(1)} %get-tuple-element.90, pred[512,512]{0,1:T(8,128)(4,1)S(1)} %not_and_fusion), kind=kOutput, calls=%fused_computation.20 | convolution fusion | flops 272891904 | bytes 5513216 | tf_op jit(solution)/shard_map/while/body/eval_jaxpr/gqk,gqe->kge/dot_general | solution.py:150
  50.0 1.0 copy.119
  51.0 0.0 reduce-scatter.12.cloned.1.call-update
  51.0 0.0 all-gather.4.cloned.1.call-start
  51.1 0.2 multiply_cosine_fusion
  51.3 18.0 %reduce-scatter.10.cloned.1.call-done = bf16[128,512]{1,0:T(8,128)(2,1)} async-done(((bf16[512,512]{1,0:T(8,128)(2,1)}), bf16[128,512]{1,0:T(8,128)(2,1)}) %reduce-scatter.10.cloned.1.call-update) | async-done | bytes 131088
  69.3 1.0 copy.118
  70.5 23.6 %reduce-scatter.12.cloned.1.call-done = bf16[128,512]{1,0:T(8,128)(2,1)} async-done(((bf16[512,512]{1,0:T(8,128)(2,1)}), bf16[128,512]{1,0:T(8,128)(2,1)}) %reduce-scatter.12.cloned.1.call-update) | async-done | bytes 131088
  94.0 1.0 copy.120
  95.1 0.7 pad_maximum_fusion
  95.8 0.2 reduce-scatter.8.cloned.1.call-start
  96.0 2.3 %copy.100 = bf16[1,128,4096]{1,2,0:T(8,128)(2,1)} copy(bf16[1,128,4096]{2,1,0:T(8,128)(2,1)} %param.10) | data formatting | bytes 2097152 | tf_op args[4]
  98.3 1.9 copy.101
  100.2 22.5 %all_to_all.18 = bf16[128,8,512]{0,1,2:T(8,128)(2,1)} all-to-all(bf16[128,8,512]{0,1,2:T(8,128)(2,1)S(1)} %copy.101), channel_id=1, replica_groups=mesh['dp'=8,'blk'=4] {'blk'}, dimensions={2} | all-to-all | bytes 2097152 | tf_op jit(solution)/shard_map/all_to_all | solution.py:217
  122.8 3.0 %copy.102 = bf16[128,8,512]{2,1,0:T(8,128)(2,1)} copy(bf16[128,8,512]{0,1,2:T(8,128)(2,1)} %all_to_all.18) | data formatting | bytes 2097152 | tf_op jit(solution)/shard_map/all_to_all | solution.py:217
  125.8 2.6 %copy.103 = bf16[4,128,8,128]{3,1,0,2:T(8,128)(2,1)} copy(bf16[4,128,8,128]{3,2,0,1:T(8,128)(2,1)} %bitcast.62) | data formatting | bytes 2097152 | tf_op jit(solution)/shard_map/all_to_all | solution.py:217
  128.4 4.1 %convert_bitcast_fusion = bf16[8,128,1024]{1,2,0:T(8,128)(2,1)} fusion(bf16[512,8,128]{2,0,1:T(8,128)(2,1)} %bitcast.72, bf16[512,1024]{0,1:T(8,128)(2,1)} %all-gather.4.cloned.1.call-done), kind=kOutput, calls=%fused_computation.8 | convolution fusion | flops 1074790400 | bytes 4194304 | tf_op jit(solution)/shard_map/tif,tc->ifc/dot_general | solution.py:218
  132.5 0.9 convolution_convert_fusion.1
  133.4 0.4 copy.97
  133.8 1.2 convert_element_type.78
  135.0 0.8 copy.105
  135.8 0.8 copy.104
  136.6 64.5 %reduce-scatter.8.cloned.1.call-done = bf16[1,128,1024]{1,2,0:T(8,128)(2,1)} async-done(((bf16[8,128,1024]{1,2,0:T(8,128)(2,1)}), bf16[1,128,1024]{1,2,0:T(8,128)(2,1)}) %reduce-scatter.8.cloned.1.call-update) | async-done | bytes 262160 | tf_op jit(solution)/shard_map/reduce_scatter | solution.py:225
  201.0 1.0 bitcast_convert_fusion
  202.0 1.0 copy.106
  (26 shorter events, 0.3 us)
Async XLA Ops:
  7.2 62.1 %reduce-scatter.10.cloned.1.call-start = ((), (), s32[]{:S(2)}) async-start(), calls=%async_computation.6 | async-start | bytes 655360
  22.8 3.9 %copy-start.2 = (bf16[1,128,2048]{2,1,0:T(8,128)(2,1)S(1)}, bf16[1,128,2048]{2,1,0:T(8,128)(2,1)}, u32[]{:S(2)}) copy-start(bf16[1,128,2048]{2,1,0:T(8,128)(2,1)} %param.9) | copy-start | bytes 1572868
  23.8 1.9 copy-start
  23.8 4.0 %copy-start.4 = (bf16[1,128,512]{2,1,0:T(8,128)(2,1)S(1)}, bf16[1,128,512]{2,1,0:T(8,128)(2,1)}, u32[]{:S(2)}) copy-start(bf16[1,128,512]{2,1,0:T(8,128)(2,1)} %param.8) | copy-start | bytes 393220
  27.8 12.4 %copy-start.3 = (bf16[4,512,128]{1,2,0:T(8,128)(2,1)}, bf16[4,512,128]{1,2,0:T(8,128)(2,1)S(1)}, u32[]{:S(2)}) copy-start(bf16[4,512,128]{1,2,0:T(8,128)(2,1)S(1)} %reshape.333) | copy-start | bytes 1572868
  35.3 4.9 %copy-start.1 = (f32[4,512,512]{1,2,0:T(8,128)S(1)}, f32[4,512,512]{1,2,0:T(8,128)}, u32[]{:S(2)}) copy-start(f32[4,512,512]{1,2,0:T(8,128)} %copy-done) | copy-start | bytes 12582916
  46.6 47.5 %reduce-scatter.12.cloned.1.call-start = ((), (), s32[]{:S(2)}) async-start(), calls=%async_computation.7 | async-start | bytes 655360
  51.0 77.3 %all-gather.4.cloned.1.call-start = ((), (), s32[]{:S(2)}) async-start(), calls=%async_computation.4 | async-start | bytes 1310720 | tf_op jit(solution)/shard_map/all_gather | solution.py:221
  95.8 105.2 %reduce-scatter.8.cloned.1.call-start = ((), (), s32[]{:S(2)}) async-start(), calls=%async_computation.5 | async-start | bytes 2359296 | tf_op jit(solution)/shard_map/reduce_scatter | solution.py:225
Sparse Core Ops, SparseCore 0:
  46.7 22.5 reduce-scatter.9
  72.4 21.6 reduce-scatter.11
  96.2 22.0 all-gather.3
  132.6 68.3 reduce-scatter.7
where the time goes:
time: 210 us
  waiting for transfers between devices  106 us (50%)
  blocking collectives  38.5 us (18%)
  local copies, waits for them, and re-layouts  26.8 us (13%)
  matrix products  18.5 us (9%)
  between operations  15.3 us (7%)
  other arithmetic  3.97 us (2%)
    reduce_scatter x1, waiting for transfers between devices, body(): lax.psum_scatter(sequence_weight.astype(jnp.bfloat16), 'dp', scatter_dime...  64.5 us
    unnamed x6, waiting for transfers between devices  41.6 us
    all_to_all x1, blocking collectives, body(): lax.all_to_all(grouped_input, 'blk', split_axis=2, concat_axis=0, tiled=T...  22.5 us
    unnamed x20, local copies, waits for them, and re-layouts  13 us
    all_gather x1, blocking collectives, body(): lax.all_gather(keys[0], 'blk', axis=0, tiled=True)  8.68 us
    all_gather x1, blocking collectives, body(): lax.all_gather(values[0], 'blk', axis=0, tiled=True)  7.29 us
    all_to_all x2, local copies, waits for them, and re-layouts, body(): lax.all_to_all(grouped_input, 'blk', split_axis=2, concat_axis=0, tiled=T...  5.62 us
    dot_general x1, matrix products, forward_block(): jnp.einsum('gqk,kge->gqe', weights, value_heads, precision=lax.Precision....  4.93 us
  transfers between devices with their start and end apart: 4, of which 3 were waited for; matrix products, arithmetic and copies ran while one was open for 9% of the time, Pallas kernels for 0%

commit v1 on v0

--- a/solution.py
+++ b/solution.py
@@ -1,8 +1,12 @@
+import functools
 import math
 
 import jax
 import jax.numpy as jnp
+import numpy as np
 from jax import lax
+from jax.experimental import pallas as pl
+from jax.experimental.pallas import tpu as pltpu
 from jax.sharding import PartitionSpec as P
 
 HEAD = 128
@@ -231,6 +235,337 @@
     return (query_grad[None], key_out[None], value_out[None], weight_grad)
 
 
+def flipped(coordinate, bit):
+    return 1 - coordinate if bit else coordinate
+
+
+def fused_kernel(
+    sizes, len_ref, q_ref, k_ref, v_ref, o_ref, x_ref, cos_ref, sin_ref,
+    qg_ref, kg_ref, vg_ref, w_ref,
+    qbuf, obuf, kbuf, vbuf, dqbuf, acc, part, precv, kgbuf, gbuf, xin, xt, wbuf, zrecv,
+    local_sem, send_sem, recv_sem,
+):
+    rows, local_heads, group, shards, depth = sizes
+    seq = rows * shards
+    half = rows // 2
+    kv_heads = 2 * local_heads
+    kv_cols = local_heads * HEAD
+    head_cols = group * HEAD
+    q_cols = local_heads * head_cols
+    scale = 1.0 / math.sqrt(HEAD)
+    dp, b = lax.axis_index("dp"), lax.axis_index("blk")
+    z, x = dp // 2, dp % 2
+    y, c = b // 2, b % 2
+
+    def peer(rx, ry, rc):
+        px, py, pc = flipped(x, rx), flipped(y, ry), flipped(c, rc)
+        return px, py, pc
+
+    def target(rx, ry, rc):
+        px, py, pc = peer(rx, ry, rc)
+        return (2 * z + px, 2 * py + pc)
+
+    counts = {"local": 0, "remote": 0}
+    pending = []
+
+    def local(src, dst):
+        at = counts["local"]
+        counts["local"] += 1
+        copy = pltpu.make_async_copy(src, dst, local_sem.at[at])
+        copy.start()
+        return copy
+
+    def remote(src, dst, landing, device):
+        at = counts["remote"]
+        counts["remote"] += 1
+        copy = pltpu.make_async_remote_copy(
+            src_ref=src, dst_ref=dst, send_sem=send_sem.at[at], recv_sem=recv_sem.at[at],
+            device_id=device, device_id_type=pl.DeviceIdType.MESH,
+        )
+        copy.start()
+        pending.append(copy)
+        return pltpu.make_async_remote_copy(
+            src_ref=src, dst_ref=landing, send_sem=send_sem.at[at], recv_sem=recv_sem.at[at],
+            device_id=device, device_id_type=pl.DeviceIdType.MESH,
+        )
+
+    def cols(start, count):
+        return pl.ds(pl.multiple_of(start, HEAD), count)
+
+    def rows_of(shard):
+        return pl.ds(pl.multiple_of(shard * rows, rows), rows)
+
+    flips = [(rx, ry, rc) for rx in (0, 1) for ry in (0, 1) for rc in (0, 1)]
+    barrier = pltpu.get_barrier_semaphore()
+    for flip in flips[1:]:
+        pl.semaphore_signal(
+            barrier, inc=1, device_id=target(*flip), device_id_type=pl.DeviceIdType.MESH
+        )
+    for offset in range(1, depth):
+        pl.semaphore_signal(
+            barrier, inc=1, device_id=(2 * ((z + offset) % depth) + x, b),
+            device_id_type=pl.DeviceIdType.MESH,
+        )
+    own = [
+        local(k_ref.at[:, cols(c * kv_cols, kv_cols)], kbuf.at[b]),
+        local(v_ref.at[:, cols(c * kv_cols, kv_cols)], vbuf.at[b]),
+        local(q_ref.at[:, cols(c * q_cols, q_cols)], qbuf.at[c]),
+        local(o_ref.at[:, cols(c * q_cols, q_cols)], obuf.at[c]),
+    ]
+    group_at = x * shards + b
+
+    def features(zz, px, py, pc):
+        return cols(((2 * zz + px) * shards + 2 * py + pc) * HEAD, HEAD)
+
+    own_x = [
+        local(x_ref.at[:, features(zz, x, y, c)], xin.at[zz, group_at]) for zz in range(depth)
+    ]
+    pl.semaphore_wait(barrier, 7 + depth - 1)
+
+    first = []
+    for flip in ((0, 1, 0), (0, 1, 1), (0, 0, 1)):
+        _, py, pc = peer(*flip)
+        other = 2 * py + pc
+        for ref, buf in ((k_ref, kbuf), (v_ref, vbuf)):
+            first.append(
+                remote(ref.at[:, cols(pc * kv_cols, kv_cols)], buf.at[b], buf.at[other], target(*flip))
+            )
+    for ref, buf in ((q_ref, qbuf), (o_ref, obuf)):
+        first.append(
+            remote(
+                ref.at[:, cols((1 - c) * q_cols, q_cols)], buf.at[c], buf.at[1 - c], target(0, 0, 1)
+            )
+        )
+    for copy in own:
+        copy.wait()
+    for copy in first:
+        copy.wait_recv()
+    exchange = []
+    for flip in flips[1:]:
+        px, py, pc = peer(*flip)
+        other = px * shards + 2 * py + pc
+        for zz in range(depth):
+            exchange.append(
+                remote(
+                    x_ref.at[:, features(zz, px, py, pc)], xin.at[zz, group_at],
+                    xin.at[zz, other], target(*flip),
+                )
+            )
+
+    prompt_len, chosen_len = len_ref[0, 0], len_ref[0, 1]
+    reject_start = prompt_len + chosen_len
+    key_row = lax.broadcasted_iota(jnp.int32, (seq, 1), 0)
+    key_pos = stored_positions(key_row, rows, shards)
+    chosen = jnp.logical_and(key_pos >= prompt_len, key_pos < reject_start)
+    key_end = jnp.where(chosen, reject_start, 2 * seq)
+    lane_row = lax.broadcasted_iota(jnp.int32, (1, head_cols), 1) % rows
+    part_copies, out_copies = [], []
+    for i in range(local_heads):
+        keys = kbuf[:, :, i * HEAD : (i + 1) * HEAD].reshape(seq, HEAD)
+        values = vbuf[:, :, i * HEAD : (i + 1) * HEAD].reshape(seq, HEAD)
+        acc[...] = jnp.zeros_like(acc)
+
+        def unit(a, carry):
+            shard = 2 * y + a
+            low = shard * half
+            high = (2 * shards - 1 - shard) * half
+            query_pos = jnp.where(lane_row >= half, high - half + lane_row, low + lane_row)
+            starts = [(i * group + h) * HEAD for h in range(group)]
+            queries = jnp.concatenate([qbuf[a, :, s : s + HEAD] for s in starts], axis=0)
+            grads = jnp.concatenate([obuf[a, :, s : s + HEAD] for s in starts], axis=0)
+            last = (((1,), (1,)), ((), ()))
+            first_dims = (((0,), (0,)), ((), ()))
+            scores = lax.dot_general(keys, queries, last, preferred_element_type=jnp.float32)
+            prob_grad = lax.dot_general(values, grads, last, preferred_element_type=jnp.float32)
+            allowed = jnp.logical_and(key_pos <= query_pos, query_pos < key_end)
+            scores = jnp.where(allowed, scores, masked_fill)
+            top = jnp.max(scores, axis=0, keepdims=True)
+            weights = jnp.exp((scores - top) * scale)
+            inverse = 1.0 / jnp.sum(weights, axis=0, keepdims=True)
+            delta = jnp.sum(weights * prob_grad, axis=0, keepdims=True) * inverse
+            probs = (weights * inverse).astype(jnp.bfloat16)
+            score_grad = (weights * (prob_grad - delta) * (scale * inverse)).astype(jnp.bfloat16)
+            acc[:, :HEAD] += jnp.dot(score_grad, queries, preferred_element_type=jnp.float32)
+            acc[:, HEAD:] += jnp.dot(probs, grads, preferred_element_type=jnp.float32)
+            query_grad = lax.dot_general(
+                score_grad, keys, first_dims, preferred_element_type=jnp.float32
+            ).astype(jnp.bfloat16)
+            for h in range(group):
+                dqbuf[i, a, :, h * HEAD : (h + 1) * HEAD] = query_grad[h * rows : (h + 1) * rows]
+            return carry
+
+        lax.fori_loop(0, 2, unit, 0)
+        part[i] = acc[...].astype(jnp.bfloat16)
+        part_copies.append(remote(part.at[i], precv.at[i], precv.at[i], target(0, 1, 0)))
+        own_cols = cols((c * local_heads + i) * head_cols, head_cols)
+        other_cols = cols(((1 - c) * local_heads + i) * head_cols, head_cols)
+        out_copies.append(
+            remote(
+                dqbuf.at[i, 1 - c], qg_ref.at[:, own_cols], qg_ref.at[:, other_cols], target(0, 0, 1)
+            )
+        )
+        own.append(local(dqbuf.at[i, c], qg_ref.at[:, own_cols]))
+
+    for copy in own_x:
+        copy.wait()
+    for copy in exchange:
+        copy.wait_recv()
+    for zz in range(depth):
+        for at in range(2 * shards):
+            xt[zz, :, at * rows : (at + 1) * rows] = xin[zz, at].T
+
+    sibling = 2 * y + 1 - c
+    to_x, to_sibling = [], []
+    for i in range(local_heads):
+        part_copies[i].wait_recv()
+        total = part[i].astype(jnp.float32) + precv[i].astype(jnp.float32)
+        key_sum, value_sum = total[:, :HEAD], total[:, HEAD:]
+        kgbuf[i] = key_sum.astype(jnp.bfloat16)
+        g, other_g = c * local_heads + i, (1 - c) * local_heads + i
+        turned = pltpu.roll(key_sum, HEAD // 2, 1)
+        gbuf[g, x, :, :HEAD] = (key_sum * cos_ref[...] + turned * sin_ref[...]).astype(jnp.bfloat16)
+        gbuf[g, x, :, HEAD:] = value_sum.astype(jnp.bfloat16)
+        to_x.append(remote(gbuf.at[g, x], gbuf.at[g, x], gbuf.at[g, 1 - x], target(1, 0, 0)))
+        to_sibling.append(
+            remote(gbuf.at[g, x], gbuf.at[g, x], gbuf.at[other_g, x], target(0, 0, 1))
+        )
+        own_cols, other_cols = cols(g * HEAD, HEAD), cols(other_g * HEAD, HEAD)
+        for buf, out in (
+            (kgbuf.at[i], kg_ref),
+            (gbuf.at[g, x, :, HEAD : 2 * HEAD], vg_ref),
+        ):
+            own.append(local(buf.at[rows_of(b), :], out.at[:, own_cols]))
+            out_copies.append(
+                remote(
+                    buf.at[rows_of(sibling), :], out.at[:, own_cols], out.at[:, other_cols],
+                    target(0, 0, 1),
+                )
+            )
+
+    scattered = []
+    for i in range(local_heads):
+        g, other_g = c * local_heads + i, (1 - c) * local_heads + i
+        to_x[i].wait_recv()
+        relayed = remote(
+            gbuf.at[g, 1 - x], gbuf.at[g, 1 - x], gbuf.at[other_g, 1 - x], target(0, 0, 1)
+        )
+        to_sibling[i].wait_recv()
+        relayed.wait_recv()
+        for j in range(2):
+            grad_cols = gbuf[j * local_heads + i].reshape(2 * seq, 2 * HEAD)
+            for zz in range(depth):
+                wbuf[i, zz, :, j * 2 * HEAD : (j + 1) * 2 * HEAD] = jnp.dot(
+                    xt[zz], grad_cols, preferred_element_type=jnp.float32
+                ).astype(jnp.bfloat16)
+        for offset in range(1, depth):
+            far = (z + offset) % depth
+            scattered.append(
+                remote(
+                    wbuf.at[i, far], zrecv.at[i, offset - 1], zrecv.at[i, offset - 1],
+                    (2 * far + x, b),
+                )
+            )
+
+    for i in range(local_heads):
+        total = wbuf[i, z].astype(jnp.float32)
+        for offset in range(1, depth):
+            scattered[i * (depth - 1) + offset - 1].wait_recv()
+            total = total + zrecv[i, offset - 1].astype(jnp.float32)
+        for j in range(2):
+            g = j * local_heads + i
+            for kind in range(2):
+                at = kind * kv_heads * HEAD + g * HEAD
+                piece = (2 * j + kind) * HEAD
+                w_ref[:, at : at + HEAD] = total[:, piece : piece + HEAD]
+    for copy in own[4:]:
+        copy.wait()
+    for copy in out_copies:
+        copy.wait_recv()
+    for copy in pending:
+        copy.wait_send()
+
+
+def fused_body(queries, keys, values, out_grad, layer_input, lengths):
+    shards = lax.axis_size("blk")
+    depth = lax.axis_size("dp") // 2
+    rows = queries.shape[1]
+    kv_heads = keys.shape[2] // HEAD
+    local_heads = kv_heads // 2
+    group = queries.shape[2] // keys.shape[2]
+    seq = rows * shards
+    half_dim = HEAD // 2
+    stored = np.arange(seq)
+    block = stored // (rows // 2)
+    holder = block // 2
+    block = np.where(block % 2 == 1, 2 * shards - 1 - holder, holder)
+    positions = (block * (rows // 2) + stored % (rows // 2)).astype(np.float32)
+    frequency = np.exp(
+        -(np.float32(2.0) * np.arange(half_dim, dtype=np.float32) / np.float32(HEAD))
+        * np.float32(math.log(rope_base))
+    ).astype(np.float32)
+    angles = positions[:, None] * frequency[None, :]
+    cosine = np.concatenate([np.cos(angles), np.cos(angles)], axis=1).astype(np.float32)
+    sine = np.concatenate([np.sin(angles), -np.sin(angles)], axis=1).astype(np.float32)
+    vmem = pl.BlockSpec(memory_space=pltpu.VMEM)
+    anywhere = pl.BlockSpec(memory_space=pl.ANY)
+    half = jnp.bfloat16
+    q_cols = local_heads * group * HEAD
+    kv_cols = local_heads * HEAD
+    remote_count = 8 + 7 * depth + 2 * local_heads + 4 * local_heads + local_heads
+    remote_count += local_heads * (depth - 1)
+    local_count = 4 + depth + 3 * local_heads
+    features = layer_input.shape[2] // (2 * depth * shards)
+    assert features == HEAD
+    outs = pl.pallas_call(
+        functools.partial(fused_kernel, (rows, local_heads, group, shards, depth)),
+        out_shape=(
+            jax.ShapeDtypeStruct(queries.shape[1:], half),
+            jax.ShapeDtypeStruct(keys.shape[1:], half),
+            jax.ShapeDtypeStruct(values.shape[1:], half),
+            jax.ShapeDtypeStruct((features, 2 * kv_heads * HEAD), jnp.float32),
+        ),
+        in_specs=[pl.BlockSpec(memory_space=pltpu.SMEM)] + [anywhere] * 5 + [vmem] * 2,
+        out_specs=(vmem,) * 4,
+        scratch_shapes=[
+            pltpu.VMEM((2, rows, q_cols), half),
+            pltpu.VMEM((2, rows, q_cols), half),
+            pltpu.VMEM((shards, rows, kv_cols), half),
+            pltpu.VMEM((shards, rows, kv_cols), half),
+            pltpu.VMEM((local_heads, 2, rows, group * HEAD), half),
+            pltpu.VMEM((seq, 2 * HEAD), jnp.float32),
+            pltpu.VMEM((local_heads, seq, 2 * HEAD), half),
+            pltpu.VMEM((local_heads, seq, 2 * HEAD), half),
+            pltpu.VMEM((local_heads, seq, HEAD), half),
+            pltpu.VMEM((kv_heads, 2, seq, 2 * HEAD), half),
+            pltpu.VMEM((depth, 2 * shards, rows, features), half),
+            pltpu.VMEM((depth, features, 2 * seq), half),
+            pltpu.VMEM((local_heads, depth, features, 4 * HEAD), half),
+            pltpu.VMEM((local_heads, depth - 1, features, 4 * HEAD), half),
+            pltpu.SemaphoreType.DMA((local_count,)),
+            pltpu.SemaphoreType.DMA((remote_count,)),
+            pltpu.SemaphoreType.DMA((remote_count,)),
+        ],
+        compiler_params=pltpu.CompilerParams(
+            collective_id=0, has_side_effects=True, vmem_limit_bytes=56 * 1024 * 1024
+        ),
+    )(
+        lengths, queries[0], keys[0], values[0], out_grad[0], layer_input[0],
+        jnp.asarray(cosine), jnp.asarray(sine),
+    )
+    query_grad, key_grad, value_grad, weight_grad = outs
+    return (query_grad[None], key_grad[None], value_grad[None], weight_grad)
+
+
+def chosen_body(queries, keys, values, out_grad, layer_input, lengths):
+    shards, replicas = lax.axis_size("blk"), lax.axis_size("dp")
+    paired = shards == 2 * 2 and replicas % 2 == 0 and replicas > 2
+    kv_heads = keys.shape[2] // HEAD
+    even = kv_heads % 2 == 0 and queries.shape[1] % HEAD == 0
+    if paired and even and layer_input.shape[2] == replicas * shards * HEAD:
+        return fused_body(queries, keys, values, out_grad, layer_input, lengths)
+    return body(queries, keys, values, out_grad, layer_input, lengths)
+
+
 def solution(mesh):
     placed = (
         P("dp", "blk", None),
@@ -241,7 +576,7 @@
         P("dp", None),
     )
     return jax.shard_map(
-        body,
+        chosen_body,
         mesh=mesh,
         in_specs=placed,
         out_specs=(

time: 210 us -> 71.6 us (0.34)
  waiting for transfers between devices: 106 us -> 0 us
  Pallas kernels: 0 us -> 65.3 us
  blocking collectives: 38.5 us -> 0 us
  local copies, waits for them, and re-layouts: 26.8 us -> 4.35 us
  matrix products: 18.5 us -> 0 us
  between operations: 15.3 us -> 0.66 us
  other arithmetic: 3.97 us -> 0 us
    pallas_call x0 -> x1, Pallas kernels: none -> 65.3 us  [fused_body(): pl.pallas_call(functools.partial(fused_kernel, (rows, local_heads, group,...]
    reduce_scatter x1 -> x0, waiting for transfers between devices: 64.5 us -> none  [body(): lax.psum_scatter(sequence_weight.astype(jnp.bfloat16), 'dp', scatter_dime...]
    unnamed x6 -> x0, waiting for transfers between devices: 41.6 us -> none
    all_to_all x1 -> x0, blocking collectives: 22.5 us -> none  [body(): lax.all_to_all(grouped_input, 'blk', split_axis=2, concat_axis=0, tiled=T...]
    dot_general x7 -> x0, matrix products: 18.5 us -> none  [the longest x1 4.93 us: forward_block(): jnp.einsum('gqk,kge->gqe', weights, value_heads, precision=lax.Precision....]
    all_gather x2 -> x0, blocking collectives: 16 us -> none  [the longest x1 8.68 us: body(): lax.all_gather(keys[0], 'blk', axis=0, tiled=True)]
    unnamed x20 -> x10, local copies, waits for them, and re-layouts: 13 us -> 4.35 us
    all_to_all x2 -> x0, local copies, waits for them, and re-layouts: 5.62 us -> none  [body(): lax.all_to_all(grouped_input, 'blk', split_axis=2, concat_axis=0, tiled=T...]
  transfers between devices with their start and end apart: 4 -> 0, of which waited for: 3 -> 0; matrix products, arithmetic and copies ran while one was open for 9% -> 0% of each run, Pallas kernels for 0% -> 0%
where the time goes in v1:
time: 71.6 us; the launch traced here: 70.3 us
  Pallas kernels  65.3 us (91%)
  local copies, waits for them, and re-layouts  4.35 us (6%)
    pallas_call x1, Pallas kernels, fused_body(): pl.pallas_call(functools.partial(fused_kernel, (rows, local_heads, group,...  65.3 us
    unnamed x10, local copies, waits for them, and re-layouts  4.35 us

profile of v1, /device:TPU:0, one launch (start us, length us, event | category | flops | bytes accessed | tf_op | source)
XLA Modules:
  0.0 70.3 jit_solution(14208415069299983989)
XLA Ops:
  0.6 65.3 %shard_map.111 = (bf16[128,2048]{1,0:T(8,128)(2,1)}, bf16[128,512]{1,0:T(8,128)(2,1)}, bf16[128,512]{1,0:T(8,128)(2,1)}, f32[128,1024]{1,0:T(8,128)}) custom-call(s32[1,3]{1,0:T(1,128)} %len_ref.1, bf16[128,2048]{1,0:T(8,128)(2,1)} %bitcast.10, bf16[128,512]{1,0:T(8,128)(2,1)} %bitcast.12, bf16[128,512]{1,0:T(8,128)(2,1)} %bitcast.13, ...), custom_call_target="tpu_custom_call" | custom-call | tf_op jit(solution)/shard_map/pallas_call | solution.py:519
  65.9 0.0 copy-start.2
  65.9 0.0 copy-start
  65.9 1.9 %copy.16 = bf16[1,128,2048]{2,1,0:T(8,128)(2,1)} copy(bf16[1,128,2048]{2,1,0:T(8,128)(2,1)} %bitcast.9) | data formatting | bytes 1048576
  67.9 0.0 copy-done.2
  67.9 0.0 copy-start.1
  67.9 0.7 copy.17
  68.5 0.3 copy-done.1
  68.8 0.7 copy.18
  69.5 0.0 copy-done
  69.5 0.8 %copy.19 = f32[128,1024]{1,0:T(8,128)} copy(f32[128,1024]{1,0:T(8,128)S(1)} %copy-done) | data formatting | bytes 1048576
Async XLA Ops:
  65.9 2.0 %copy-start.2 = (bf16[128,512]{1,0:T(8,128)(2,1)S(1)}, bf16[128,512]{1,0:T(8,128)(2,1)}, u32[]{:S(2)}) copy-start(bf16[128,512]{1,0:T(8,128)(2,1)} %get-tuple-element.9) | copy-start | bytes 393220
  65.9 3.6 %copy-start = (f32[128,1024]{1,0:T(8,128)S(1)}, f32[128,1024]{1,0:T(8,128)}, u32[]{:S(2)}) copy-start(f32[128,1024]{1,0:T(8,128)} %get-tuple-element.19) | copy-start | bytes 1572868
  67.9 1.0 %copy-start.1 = (bf16[128,512]{1,0:T(8,128)(2,1)S(1)}, bf16[128,512]{1,0:T(8,128)(2,1)}, u32[]{:S(2)}) copy-start(bf16[128,512]{1,0:T(8,128)(2,1)} %get-tuple-element.10) | copy-start | bytes 393220

commit v2 on v1

--- a/solution.py
+++ b/solution.py
@@ -242,16 +242,14 @@
 def fused_kernel(
     sizes, len_ref, q_ref, k_ref, v_ref, o_ref, x_ref, cos_ref, sin_ref,
     qg_ref, kg_ref, vg_ref, w_ref,
-    qbuf, obuf, kbuf, vbuf, dqbuf, acc, part, precv, kgbuf, gbuf, xin, xt, wbuf, zrecv,
+    qbuf, obuf, kbuf, vbuf, dqbuf, acc, part, precv, kgbuf, gbuf, xin, xt, wbuf, zrecv, wown,
     local_sem, send_sem, recv_sem,
 ):
     rows, local_heads, group, shards, depth = sizes
     seq = rows * shards
     half = rows // 2
     kv_heads = 2 * local_heads
-    kv_cols = local_heads * HEAD
     head_cols = group * HEAD
-    q_cols = local_heads * head_cols
     scale = 1.0 / math.sqrt(HEAD)
     dp, b = lax.axis_index("dp"), lax.axis_index("blk")
     z, x = dp // 2, dp % 2
@@ -301,17 +299,24 @@
         pl.semaphore_signal(
             barrier, inc=1, device_id=target(*flip), device_id_type=pl.DeviceIdType.MESH
         )
-    for offset in range(1, depth):
+    moves = [(1, 1), (0, 1), (1, 0), (0, 0)]
+
+    def moved(outer, inner):
+        return 2 * flipped(z // 2, outer) + flipped(z % 2, inner)
+
+    for move in moves[:-1]:
         pl.semaphore_signal(
-            barrier, inc=1, device_id=(2 * ((z + offset) % depth) + x, b),
+            barrier, inc=1, device_id=(2 * moved(*move) + x, b),
             device_id_type=pl.DeviceIdType.MESH,
         )
-    own = [
-        local(k_ref.at[:, cols(c * kv_cols, kv_cols)], kbuf.at[b]),
-        local(v_ref.at[:, cols(c * kv_cols, kv_cols)], vbuf.at[b]),
-        local(q_ref.at[:, cols(c * q_cols, q_cols)], qbuf.at[c]),
-        local(o_ref.at[:, cols(c * q_cols, q_cols)], obuf.at[c]),
-    ]
+    own = []
+    for i in range(local_heads):
+        at = c * local_heads + i
+        own.append(local(k_ref.at[:, cols(at * HEAD, HEAD)], kbuf.at[i, b]))
+        own.append(local(v_ref.at[:, cols(at * HEAD, HEAD)], vbuf.at[i, b]))
+        own.append(local(q_ref.at[:, cols(at * head_cols, head_cols)], qbuf.at[i, c]))
+        own.append(local(o_ref.at[:, cols(at * head_cols, head_cols)], obuf.at[i, c]))
+    own_count = len(own)
     group_at = x * shards + b
 
     def features(zz, px, py, pc):
@@ -320,37 +325,41 @@
     own_x = [
         local(x_ref.at[:, features(zz, x, y, c)], xin.at[zz, group_at]) for zz in range(depth)
     ]
-    pl.semaphore_wait(barrier, 7 + depth - 1)
+    pl.semaphore_wait(barrier, len(flips) - 1 + len(moves) - 1)
 
     first = []
-    for flip in ((0, 1, 0), (0, 1, 1), (0, 0, 1)):
-        _, py, pc = peer(*flip)
-        other = 2 * py + pc
-        for ref, buf in ((k_ref, kbuf), (v_ref, vbuf)):
-            first.append(
-                remote(ref.at[:, cols(pc * kv_cols, kv_cols)], buf.at[b], buf.at[other], target(*flip))
+    for i in range(local_heads):
+        arriving = []
+        for flip in ((0, 1, 0), (0, 1, 1), (0, 0, 1)):
+            _, py, pc = peer(*flip)
+            other = 2 * py + pc
+            columns = cols((pc * local_heads + i) * HEAD, HEAD)
+            for ref, buf in ((k_ref, kbuf), (v_ref, vbuf)):
+                arriving.append(
+                    remote(ref.at[:, columns], buf.at[i, b], buf.at[i, other], target(*flip))
+                )
+        columns = cols(((1 - c) * local_heads + i) * head_cols, head_cols)
+        for ref, buf in ((q_ref, qbuf), (o_ref, obuf)):
+            arriving.append(
+                remote(ref.at[:, columns], buf.at[i, c], buf.at[i, 1 - c], target(0, 0, 1))
             )
-    for ref, buf in ((q_ref, qbuf), (o_ref, obuf)):
-        first.append(
-            remote(
-                ref.at[:, cols((1 - c) * q_cols, q_cols)], buf.at[c], buf.at[1 - c], target(0, 0, 1)
-            )
-        )
-    for copy in own:
-        copy.wait()
-    for copy in first:
-        copy.wait_recv()
-    exchange = []
-    for flip in flips[1:]:
-        px, py, pc = peer(*flip)
-        other = px * shards + 2 * py + pc
-        for zz in range(depth):
-            exchange.append(
+        first.append(arriving)
+    exchange = {}
+
+    def send_features(move):
+        zz = moved(*move)
+        arriving = []
+        for flip in flips[1:]:
+            px, py, pc = peer(*flip)
+            other = px * shards + 2 * py + pc
+            arriving.append(
                 remote(
                     x_ref.at[:, features(zz, px, py, pc)], xin.at[zz, group_at],
                     xin.at[zz, other], target(*flip),
                 )
             )
+        exchange[move] = arriving
+
 
     prompt_len, chosen_len = len_ref[0, 0], len_ref[0, 1]
     reject_start = prompt_len + chosen_len
@@ -361,8 +370,16 @@
     lane_row = lax.broadcasted_iota(jnp.int32, (1, head_cols), 1) % rows
     part_copies, out_copies = [], []
     for i in range(local_heads):
-        keys = kbuf[:, :, i * HEAD : (i + 1) * HEAD].reshape(seq, HEAD)
-        values = vbuf[:, :, i * HEAD : (i + 1) * HEAD].reshape(seq, HEAD)
+        per_head = own_count // local_heads
+        for copy in own[i * per_head : (i + 1) * per_head]:
+            copy.wait()
+        for copy in first[i]:
+            copy.wait_recv()
+        if i == 0:
+            send_features(moves[0])
+            send_features(moves[1])
+        keys = kbuf[i].reshape(seq, HEAD)
+        values = vbuf[i].reshape(seq, HEAD)
         acc[...] = jnp.zeros_like(acc)
 
         def unit(a, carry):
@@ -370,9 +387,9 @@
             low = shard * half
             high = (2 * shards - 1 - shard) * half
             query_pos = jnp.where(lane_row >= half, high - half + lane_row, low + lane_row)
-            starts = [(i * group + h) * HEAD for h in range(group)]
-            queries = jnp.concatenate([qbuf[a, :, s : s + HEAD] for s in starts], axis=0)
-            grads = jnp.concatenate([obuf[a, :, s : s + HEAD] for s in starts], axis=0)
+            starts = [h * HEAD for h in range(group)]
+            queries = jnp.concatenate([qbuf[i, a, :, s : s + HEAD] for s in starts], axis=0)
+            grads = jnp.concatenate([obuf[i, a, :, s : s + HEAD] for s in starts], axis=0)
             last = (((1,), (1,)), ((), ()))
             first_dims = (((0,), (0,)), ((), ()))
             scores = lax.dot_general(keys, queries, last, preferred_element_type=jnp.float32)
@@ -397,6 +414,10 @@
         lax.fori_loop(0, 2, unit, 0)
         part[i] = acc[...].astype(jnp.bfloat16)
         part_copies.append(remote(part.at[i], precv.at[i], precv.at[i], target(0, 1, 0)))
+        if i == 0:
+            send_features(moves[2])
+        if i == local_heads - 1:
+            send_features(moves[3])
         own_cols = cols((c * local_heads + i) * head_cols, head_cols)
         other_cols = cols(((1 - c) * local_heads + i) * head_cols, head_cols)
         out_copies.append(
@@ -408,15 +429,25 @@
 
     for copy in own_x:
         copy.wait()
-    for copy in exchange:
-        copy.wait_recv()
-    for zz in range(depth):
+    ready = set()
+
+    def turn_features(move):
+        if move in ready:
+            return
+        ready.add(move)
+        zz = moved(*move)
+        for copy in exchange[move]:
+            copy.wait_recv()
         for at in range(2 * shards):
             xt[zz, :, at * rows : (at + 1) * rows] = xin[zz, at].T
 
+    turn_features(moves[0])
+    turn_features(moves[1])
     sibling = 2 * y + 1 - c
     to_x, to_sibling = [], []
     for i in range(local_heads):
+        if i == local_heads - 1:
+            turn_features(moves[2])
         part_copies[i].wait_recv()
         total = part[i].astype(jnp.float32) + precv[i].astype(jnp.float32)
         key_sum, value_sum = total[:, :HEAD], total[:, HEAD:]
@@ -442,7 +473,11 @@
                 )
             )
 
-    scattered = []
+    def z_target(move):
+        return (2 * moved(*move) + x, b)
+
+    crossed, direct = [], []
+    turn_features(moves[3])
     for i in range(local_heads):
         g, other_g = c * local_heads + i, (1 - c) * local_heads + i
         to_x[i].wait_recv()
@@ -451,33 +486,39 @@
         )
         to_sibling[i].wait_recv()
         relayed.wait_recv()
+
+        def product(move, j):
+            grad_cols = gbuf[j * local_heads + i].reshape(2 * seq, 2 * HEAD)
+            return jnp.dot(xt[moved(*move)], grad_cols, preferred_element_type=jnp.float32)
+
+        halves = [slice(j * 2 * HEAD, (j + 1) * 2 * HEAD) for j in range(2)]
         for j in range(2):
-            grad_cols = gbuf[j * local_heads + i].reshape(2 * seq, 2 * HEAD)
-            for zz in range(depth):
-                wbuf[i, zz, :, j * 2 * HEAD : (j + 1) * 2 * HEAD] = jnp.dot(
-                    xt[zz], grad_cols, preferred_element_type=jnp.float32
-                ).astype(jnp.bfloat16)
-        for offset in range(1, depth):
-            far = (z + offset) % depth
-            scattered.append(
-                remote(
-                    wbuf.at[i, far], zrecv.at[i, offset - 1], zrecv.at[i, offset - 1],
-                    (2 * far + x, b),
-                )
-            )
+            wbuf[i, 0, :, halves[j]] = product((1, 1), j).astype(jnp.bfloat16)
+        before = remote(wbuf.at[i, 0], zrecv.at[i, 0], zrecv.at[i, 0], z_target((0, 1)))
+        for j in range(2):
+            wbuf[i, 1, :, halves[j]] = product((0, 1), j).astype(jnp.bfloat16)
+        direct.append(remote(wbuf.at[i, 1], zrecv.at[i, 1], zrecv.at[i, 1], z_target((0, 1))))
+        for j in range(2):
+            wown[0, :, halves[j]] = product((1, 0), j)
+        for j in range(2):
+            wown[1 + i, :, halves[j]] = product((0, 0), j)
+        before.wait_recv()
+        wbuf[i, 2] = (wown[0] + zrecv[i, 0].astype(jnp.float32)).astype(jnp.bfloat16)
+        crossed.append(remote(wbuf.at[i, 2], zrecv.at[i, 2], zrecv.at[i, 2], z_target((1, 0))))
 
     for i in range(local_heads):
-        total = wbuf[i, z].astype(jnp.float32)
-        for offset in range(1, depth):
-            scattered[i * (depth - 1) + offset - 1].wait_recv()
-            total = total + zrecv[i, offset - 1].astype(jnp.float32)
+        direct[i].wait_recv()
+        crossed[i].wait_recv()
+        total = (
+            wown[1 + i] + zrecv[i, 1].astype(jnp.float32) + zrecv[i, 2].astype(jnp.float32)
+        )
         for j in range(2):
             g = j * local_heads + i
             for kind in range(2):
                 at = kind * kv_heads * HEAD + g * HEAD
                 piece = (2 * j + kind) * HEAD
                 w_ref[:, at : at + HEAD] = total[:, piece : piece + HEAD]
-    for copy in own[4:]:
+    for copy in own[own_count:]:
         copy.wait()
     for copy in out_copies:
         copy.wait_recv()
@@ -509,11 +550,9 @@
     vmem = pl.BlockSpec(memory_space=pltpu.VMEM)
     anywhere = pl.BlockSpec(memory_space=pl.ANY)
     half = jnp.bfloat16
-    q_cols = local_heads * group * HEAD
-    kv_cols = local_heads * HEAD
-    remote_count = 8 + 7 * depth + 2 * local_heads + 4 * local_heads + local_heads
-    remote_count += local_heads * (depth - 1)
-    local_count = 4 + depth + 3 * local_heads
+    remote_count = 8 * local_heads + 7 * depth + 2 * local_heads + 4 * local_heads + local_heads
+    remote_count += 3 * local_heads
+    local_count = 4 * local_heads + depth + 3 * local_heads
     features = layer_input.shape[2] // (2 * depth * shards)
     assert features == HEAD
     outs = pl.pallas_call(
@@ -527,10 +566,10 @@
         in_specs=[pl.BlockSpec(memory_space=pltpu.SMEM)] + [anywhere] * 5 + [vmem] * 2,
         out_specs=(vmem,) * 4,
         scratch_shapes=[
-            pltpu.VMEM((2, rows, q_cols), half),
-            pltpu.VMEM((2, rows, q_cols), half),
-            pltpu.VMEM((shards, rows, kv_cols), half),
-            pltpu.VMEM((shards, rows, kv_cols), half),
+            pltpu.VMEM((local_heads, 2, rows, group * HEAD), half),
+            pltpu.VMEM((local_heads, 2, rows, group * HEAD), half),
+            pltpu.VMEM((local_heads, shards, rows, HEAD), half),
+            pltpu.VMEM((local_heads, shards, rows, HEAD), half),
             pltpu.VMEM((local_heads, 2, rows, group * HEAD), half),
             pltpu.VMEM((seq, 2 * HEAD), jnp.float32),
             pltpu.VMEM((local_heads, seq, 2 * HEAD), half),
@@ -539,8 +578,9 @@
             pltpu.VMEM((kv_heads, 2, seq, 2 * HEAD), half),
             pltpu.VMEM((depth, 2 * shards, rows, features), half),
             pltpu.VMEM((depth, features, 2 * seq), half),
-            pltpu.VMEM((local_heads, depth, features, 4 * HEAD), half),
-            pltpu.VMEM((local_heads, depth - 1, features, 4 * HEAD), half),
+            pltpu.VMEM((local_heads, 3, features, 4 * HEAD), half),
+            pltpu.VMEM((local_heads, 3, features, 4 * HEAD), half),
+            pltpu.VMEM((1 + local_heads, features, 4 * HEAD), jnp.float32),
             pltpu.SemaphoreType.DMA((local_count,)),
             pltpu.SemaphoreType.DMA((remote_count,)),
             pltpu.SemaphoreType.DMA((remote_count,)),
@@ -558,7 +598,7 @@
 
 def chosen_body(queries, keys, values, out_grad, layer_input, lengths):
     shards, replicas = lax.axis_size("blk"), lax.axis_size("dp")
-    paired = shards == 2 * 2 and replicas % 2 == 0 and replicas > 2
+    paired = shards == 2 * 2 and replicas == 2 * shards
     kv_heads = keys.shape[2] // HEAD
     even = kv_heads % 2 == 0 and queries.shape[1] % HEAD == 0
     if paired and even and layer_input.shape[2] == replicas * shards * HEAD:

time: 71.6 us -> 67.3 us (0.940); the launches traced: 70.3 us -> 67.1 us
  Pallas kernels: 65.3 us -> 62.1 us
    pallas_call x1, Pallas kernels: 65.3 us -> 62.1 us  [fused_body(): pl.pallas_call(functools.partial(fused_kernel, (rows, local_heads, group,...]
where the time goes in v2:
time: 67.3 us; the launch traced here: 67.1 us
  Pallas kernels  62.1 us (92%)
  local copies, waits for them, and re-layouts  4.35 us (6%)
    pallas_call x1, Pallas kernels, fused_body(): pl.pallas_call(functools.partial(fused_kernel, (rows, local_heads, group,...  62.1 us
    unnamed x10, local copies, waits for them, and re-layouts  4.35 us

profile of v2, /device:TPU:0, one launch (start us, length us, event | category | flops | bytes accessed | tf_op | source)
XLA Modules:
  0.0 67.1 jit_solution(16546140344028047923)
XLA Ops:
  0.6 62.1 %shard_map.111 = (bf16[128,2048]{1,0:T(8,128)(2,1)}, bf16[128,512]{1,0:T(8,128)(2,1)}, bf16[128,512]{1,0:T(8,128)(2,1)}, f32[128,1024]{1,0:T(8,128)}) custom-call(s32[1,3]{1,0:T(1,128)} %len_ref.1, bf16[128,2048]{1,0:T(8,128)(2,1)} %bitcast.10, bf16[128,512]{1,0:T(8,128)(2,1)} %bitcast.12, bf16[128,512]{1,0:T(8,128)(2,1)} %bitcast.13, ...), custom_call_target="tpu_custom_call" | custom-call | tf_op jit(solution)/shard_map/pallas_call | solution.py:558
  62.8 0.0 copy-start.2
  62.8 0.0 copy-start
  62.8 1.9 %copy.16 = bf16[1,128,2048]{2,1,0:T(8,128)(2,1)} copy(bf16[1,128,2048]{2,1,0:T(8,128)(2,1)} %bitcast.9) | data formatting | bytes 1048576
  64.7 0.0 copy-done.2
  64.7 0.0 copy-start.1
  64.7 0.7 copy.17
  65.4 0.3 copy-done.1
  65.7 0.7 copy.18
  66.3 0.0 copy-done
  66.3 0.8 %copy.19 = f32[128,1024]{1,0:T(8,128)} copy(f32[128,1024]{1,0:T(8,128)S(1)} %copy-done) | data formatting | bytes 1048576
Async XLA Ops:
  62.8 2.0 %copy-start.2 = (bf16[128,512]{1,0:T(8,128)(2,1)S(1)}, bf16[128,512]{1,0:T(8,128)(2,1)}, u32[]{:S(2)}) copy-start(bf16[128,512]{1,0:T(8,128)(2,1)} %get-tuple-element.9) | copy-start | bytes 393220
  62.8 3.6 %copy-start = (f32[128,1024]{1,0:T(8,128)S(1)}, f32[128,1024]{1,0:T(8,128)}, u32[]{:S(2)}) copy-start(f32[128,1024]{1,0:T(8,128)} %get-tuple-element.19) | copy-start | bytes 1572868
  64.7 1.0 %copy-start.1 = (bf16[128,512]{1,0:T(8,128)(2,1)S(1)}, bf16[128,512]{1,0:T(8,128)(2,1)}, u32[]{:S(2)}) copy-start(bf16[128,512]{1,0:T(8,128)(2,1)} %get-tuple-element.10) | copy-start | bytes 393220

commit v3 on v2

--- a/solution.py
+++ b/solution.py
@@ -375,9 +375,6 @@
             copy.wait()
         for copy in first[i]:
             copy.wait_recv()
-        if i == 0:
-            send_features(moves[0])
-            send_features(moves[1])
         keys = kbuf[i].reshape(seq, HEAD)
         values = vbuf[i].reshape(seq, HEAD)
         acc[...] = jnp.zeros_like(acc)
@@ -412,12 +409,14 @@
             return carry
 
         lax.fori_loop(0, 2, unit, 0)
-        part[i] = acc[...].astype(jnp.bfloat16)
-        part_copies.append(remote(part.at[i], precv.at[i], precv.at[i], target(0, 1, 0)))
+        for kind in range(2):
+            part[i, kind] = acc[:, kind * HEAD : (kind + 1) * HEAD].astype(jnp.bfloat16)
+            part_copies.append(
+                remote(part.at[i, kind], precv.at[i, kind], precv.at[i, kind], target(0, 1, 0))
+            )
         if i == 0:
-            send_features(moves[2])
-        if i == local_heads - 1:
-            send_features(moves[3])
+            send_features(moves[0])
+            send_features(moves[1])
         own_cols = cols((c * local_heads + i) * head_cols, head_cols)
         other_cols = cols(((1 - c) * local_heads + i) * head_cols, head_cols)
         out_copies.append(
@@ -429,95 +428,91 @@
 
     for copy in own_x:
         copy.wait()
-    ready = set()
 
     def turn_features(move):
-        if move in ready:
-            return
-        ready.add(move)
         zz = moved(*move)
         for copy in exchange[move]:
             copy.wait_recv()
         for at in range(2 * shards):
             xt[zz, :, at * rows : (at + 1) * rows] = xin[zz, at].T
 
-    turn_features(moves[0])
-    turn_features(moves[1])
     sibling = 2 * y + 1 - c
+    pieces = [(i, kind) for i in range(local_heads) for kind in range(2)]
     to_x, to_sibling = [], []
-    for i in range(local_heads):
-        if i == local_heads - 1:
-            turn_features(moves[2])
-        part_copies[i].wait_recv()
-        total = part[i].astype(jnp.float32) + precv[i].astype(jnp.float32)
-        key_sum, value_sum = total[:, :HEAD], total[:, HEAD:]
-        kgbuf[i] = key_sum.astype(jnp.bfloat16)
+    for at, (i, kind) in enumerate(pieces):
+        part_copies[at].wait_recv()
+        total = part[i, kind].astype(jnp.float32) + precv[i, kind].astype(jnp.float32)
         g, other_g = c * local_heads + i, (1 - c) * local_heads + i
-        turned = pltpu.roll(key_sum, HEAD // 2, 1)
-        gbuf[g, x, :, :HEAD] = (key_sum * cos_ref[...] + turned * sin_ref[...]).astype(jnp.bfloat16)
-        gbuf[g, x, :, HEAD:] = value_sum.astype(jnp.bfloat16)
-        to_x.append(remote(gbuf.at[g, x], gbuf.at[g, x], gbuf.at[g, 1 - x], target(1, 0, 0)))
-        to_sibling.append(
-            remote(gbuf.at[g, x], gbuf.at[g, x], gbuf.at[other_g, x], target(0, 0, 1))
-        )
+        mine = gbuf.at[kind, g, x]
+        if kind == 0:
+            kgbuf[i] = total.astype(jnp.bfloat16)
+            turned = pltpu.roll(total, HEAD // 2, 1)
+            gbuf[kind, g, x] = (total * cos_ref[...] + turned * sin_ref[...]).astype(jnp.bfloat16)
+        else:
+            gbuf[kind, g, x] = total.astype(jnp.bfloat16)
+        to_x.append(remote(mine, mine, gbuf.at[kind, g, 1 - x], target(1, 0, 0)))
+        to_sibling.append(remote(mine, mine, gbuf.at[kind, other_g, x], target(0, 0, 1)))
         own_cols, other_cols = cols(g * HEAD, HEAD), cols(other_g * HEAD, HEAD)
-        for buf, out in (
-            (kgbuf.at[i], kg_ref),
-            (gbuf.at[g, x, :, HEAD : 2 * HEAD], vg_ref),
-        ):
-            own.append(local(buf.at[rows_of(b), :], out.at[:, own_cols]))
-            out_copies.append(
-                remote(
-                    buf.at[rows_of(sibling), :], out.at[:, own_cols], out.at[:, other_cols],
-                    target(0, 0, 1),
-                )
+        buf, out = (kgbuf.at[i], kg_ref) if kind == 0 else (mine, vg_ref)
+        own.append(local(buf.at[rows_of(b), :], out.at[:, own_cols]))
+        out_copies.append(
+            remote(
+                buf.at[rows_of(sibling), :], out.at[:, own_cols], out.at[:, other_cols],
+                target(0, 0, 1),
             )
+        )
+        if at == 0:
+            send_features(moves[2])
+            turn_features(moves[0])
+            turn_features(moves[1])
+        if at == 1:
+            send_features(moves[3])
 
     def z_target(move):
         return (2 * moved(*move) + x, b)
 
-    crossed, direct = [], []
-    turn_features(moves[3])
-    for i in range(local_heads):
+    before, direct, crossed = [], [], []
+
+    def cross(at):
+        before[at].wait_recv()
+        wbuf[at, 2] = (wown[at, 0] + zrecv[at, 0].astype(jnp.float32)).astype(jnp.bfloat16)
+        crossed.append(remote(wbuf.at[at, 2], zrecv.at[at, 2], zrecv.at[at, 2], z_target((1, 0))))
+
+    for at, (i, kind) in enumerate(pieces):
         g, other_g = c * local_heads + i, (1 - c) * local_heads + i
-        to_x[i].wait_recv()
-        relayed = remote(
-            gbuf.at[g, 1 - x], gbuf.at[g, 1 - x], gbuf.at[other_g, 1 - x], target(0, 0, 1)
-        )
-        to_sibling[i].wait_recv()
+        to_x[at].wait_recv()
+        theirs = gbuf.at[kind, g, 1 - x]
+        relayed = remote(theirs, theirs, gbuf.at[kind, other_g, 1 - x], target(0, 0, 1))
+        to_sibling[at].wait_recv()
         relayed.wait_recv()
-
-        def product(move, j):
-            grad_cols = gbuf[j * local_heads + i].reshape(2 * seq, 2 * HEAD)
+        grad_cols = jnp.concatenate(
+            [gbuf[kind, j * local_heads + i].reshape(2 * seq, HEAD) for j in range(2)], axis=1
+        )
+
+        def product(move):
             return jnp.dot(xt[moved(*move)], grad_cols, preferred_element_type=jnp.float32)
 
-        halves = [slice(j * 2 * HEAD, (j + 1) * 2 * HEAD) for j in range(2)]
+        wbuf[at, 0] = product((1, 1)).astype(jnp.bfloat16)
+        before.append(remote(wbuf.at[at, 0], zrecv.at[at, 0], zrecv.at[at, 0], z_target((0, 1))))
+        wbuf[at, 1] = product((0, 1)).astype(jnp.bfloat16)
+        direct.append(remote(wbuf.at[at, 1], zrecv.at[at, 1], zrecv.at[at, 1], z_target((0, 1))))
+        if at == 0:
+            turn_features(moves[2])
+        wown[at, 0] = product((1, 0))
+        if at > 0:
+            cross(at - 1)
+        if at == 0:
+            turn_features(moves[3])
+        wown[at, 1] = product((0, 0))
+    cross(len(pieces) - 1)
+
+    for at, (i, kind) in enumerate(pieces):
+        direct[at].wait_recv()
+        crossed[at].wait_recv()
+        total = wown[at, 1] + zrecv[at, 1].astype(jnp.float32) + zrecv[at, 2].astype(jnp.float32)
         for j in range(2):
-            wbuf[i, 0, :, halves[j]] = product((1, 1), j).astype(jnp.bfloat16)
-        before = remote(wbuf.at[i, 0], zrecv.at[i, 0], zrecv.at[i, 0], z_target((0, 1)))
-        for j in range(2):
-            wbuf[i, 1, :, halves[j]] = product((0, 1), j).astype(jnp.bfloat16)
-        direct.append(remote(wbuf.at[i, 1], zrecv.at[i, 1], zrecv.at[i, 1], z_target((0, 1))))
-        for j in range(2):
-            wown[0, :, halves[j]] = product((1, 0), j)
-        for j in range(2):
-            wown[1 + i, :, halves[j]] = product((0, 0), j)
-        before.wait_recv()
-        wbuf[i, 2] = (wown[0] + zrecv[i, 0].astype(jnp.float32)).astype(jnp.bfloat16)
-        crossed.append(remote(wbuf.at[i, 2], zrecv.at[i, 2], zrecv.at[i, 2], z_target((1, 0))))
-
-    for i in range(local_heads):
-        direct[i].wait_recv()
-        crossed[i].wait_recv()
-        total = (
-            wown[1 + i] + zrecv[i, 1].astype(jnp.float32) + zrecv[i, 2].astype(jnp.float32)
-        )
-        for j in range(2):
-            g = j * local_heads + i
-            for kind in range(2):
-                at = kind * kv_heads * HEAD + g * HEAD
-                piece = (2 * j + kind) * HEAD
-                w_ref[:, at : at + HEAD] = total[:, piece : piece + HEAD]
+            start = (kind * kv_heads + j * local_heads + i) * HEAD
+            w_ref[:, start : start + HEAD] = total[:, j * HEAD : (j + 1) * HEAD]
     for copy in own[own_count:]:
         copy.wait()
     for copy in out_copies:
@@ -550,9 +545,8 @@
     vmem = pl.BlockSpec(memory_space=pltpu.VMEM)
     anywhere = pl.BlockSpec(memory_space=pl.ANY)
     half = jnp.bfloat16
-    remote_count = 8 * local_heads + 7 * depth + 2 * local_heads + 4 * local_heads + local_heads
-    remote_count += 3 * local_heads
-    local_count = 4 * local_heads + depth + 3 * local_heads
+    remote_count = 7 * depth + 25 * local_heads
+    local_count = depth + 7 * local_heads
     features = layer_input.shape[2] // (2 * depth * shards)
     assert features == HEAD
     outs = pl.pallas_call(
@@ -572,15 +566,15 @@
             pltpu.VMEM((local_heads, shards, rows, HEAD), half),
             pltpu.VMEM((local_heads, 2, rows, group * HEAD), half),
             pltpu.VMEM((seq, 2 * HEAD), jnp.float32),
-            pltpu.VMEM((local_heads, seq, 2 * HEAD), half),
-            pltpu.VMEM((local_heads, seq, 2 * HEAD), half),
+            pltpu.VMEM((local_heads, 2, seq, HEAD), half),
+            pltpu.VMEM((local_heads, 2, seq, HEAD), half),
             pltpu.VMEM((local_heads, seq, HEAD), half),
-            pltpu.VMEM((kv_heads, 2, seq, 2 * HEAD), half),
+            pltpu.VMEM((2, kv_heads, 2, seq, HEAD), half),
             pltpu.VMEM((depth, 2 * shards, rows, features), half),
             pltpu.VMEM((depth, features, 2 * seq), half),
-            pltpu.VMEM((local_heads, 3, features, 4 * HEAD), half),
-            pltpu.VMEM((local_heads, 3, features, 4 * HEAD), half),
-            pltpu.VMEM((1 + local_heads, features, 4 * HEAD), jnp.float32),
+            pltpu.VMEM((2 * local_heads, 3, features, 2 * HEAD), half),
+            pltpu.VMEM((2 * local_heads, 3, features, 2 * HEAD), half),
+            pltpu.VMEM((2 * local_heads, 2, features, 2 * HEAD), jnp.float32),
             pltpu.SemaphoreType.DMA((local_count,)),
             pltpu.SemaphoreType.DMA((remote_count,)),
             pltpu.SemaphoreType.DMA((remote_count,)),

time: 67.3 us -> 67.2 us (level)
  no operation moved by 1% of the time
where the time goes in v3:
time: 67.2 us; the launch traced here: 67 us
  Pallas kernels  62 us (92%)
  local copies, waits for them, and re-layouts  4.35 us (6%)
    pallas_call x1, Pallas kernels, fused_body(): pl.pallas_call(functools.partial(fused_kernel, (rows, local_heads, group,...  62 us
    unnamed x10, local copies, waits for them, and re-layouts  4.35 us

profile of v3, /device:TPU:0, one launch (start us, length us, event | category | flops | bytes accessed | tf_op | source)
XLA Modules:
  0.0 67.0 jit_solution(15031840111760151420)
XLA Ops:
  0.6 62.0 %shard_map.111 = (bf16[128,2048]{1,0:T(8,128)(2,1)}, bf16[128,512]{1,0:T(8,128)(2,1)}, bf16[128,512]{1,0:T(8,128)(2,1)}, f32[128,1024]{1,0:T(8,128)}) custom-call(s32[1,3]{1,0:T(1,128)} %len_ref.1, bf16[128,2048]{1,0:T(8,128)(2,1)} %bitcast.10, bf16[128,512]{1,0:T(8,128)(2,1)} %bitcast.12, bf16[128,512]{1,0:T(8,128)(2,1)} %bitcast.13, ...), custom_call_target="tpu_custom_call" | custom-call | tf_op jit(solution)/shard_map/pallas_call | solution.py:552
  62.6 0.0 copy-start.2
  62.6 0.0 copy-start
  62.6 1.9 %copy.16 = bf16[1,128,2048]{2,1,0:T(8,128)(2,1)} copy(bf16[1,128,2048]{2,1,0:T(8,128)(2,1)} %bitcast.9) | data formatting | bytes 1048576
  64.6 0.0 copy-done.2
  64.6 0.0 copy-start.1
  64.6 0.7 copy.17
  65.2 0.3 copy-done.1
  65.5 0.7 copy.18
  66.2 0.0 copy-done
  66.2 0.8 %copy.19 = f32[128,1024]{1,0:T(8,128)} copy(f32[128,1024]{1,0:T(8,128)S(1)} %copy-done) | data formatting | bytes 1048576
Async XLA Ops:
  62.6 2.0 %copy-start.2 = (bf16[128,512]{1,0:T(8,128)(2,1)S(1)}, bf16[128,512]{1,0:T(8,128)(2,1)}, u32[]{:S(2)}) copy-start(bf16[128,512]{1,0:T(8,128)(2,1)} %get-tuple-element.9) | copy-start | bytes 393220
  62.6 3.6 %copy-start = (f32[128,1024]{1,0:T(8,128)S(1)}, f32[128,1024]{1,0:T(8,128)}, u32[]{:S(2)}) copy-start(f32[128,1024]{1,0:T(8,128)} %get-tuple-element.19) | copy-start | bytes 1572868
  64.6 1.0 %copy-start.1 = (bf16[128,512]{1,0:T(8,128)(2,1)S(1)}, bf16[128,512]{1,0:T(8,128)(2,1)}, u32[]{:S(2)}) copy-start(bf16[128,512]{1,0:T(8,128)(2,1)} %get-tuple-element.10) | copy-start | bytes 393220
